TPU v7x, 32 devices: a whole 2x2x4 slice. The times are simulated.
32 devices in a mesh: cfg: 2 (over x), seq: 16 (over z, y, core).
Axes of the slice: x: 2, y: 2, z: 4, core: 2. Of those that a mesh axis runs over, the one named last changes fastest.
Arguments:
- latent: bfloat16 [16, 1024, 1536], P('seq'), may hold values from -6 to 6
- text_ids: int32 [2, 512], P('cfg'), may hold values from 0 to 32127
- timestep: int32 [1], replicated, may hold values from 0 to 999
- guide_num: int32 [1], replicated, may hold values from 1024 to 8192
- guide_den: int32 [1], replicated, may hold values from 512 to 1024
- text_table: bfloat16 [32128, 1536], P('seq'), may hold values from -6 to 6
- time_in: bfloat16 [256, 1536], replicated, may hold values from -0.375 to 0.375
- time_out: bfloat16 [1536, 1536], P(None, 'seq'), may hold values from -0.15625 to 0.15625
- mod_weight: bfloat16 [1536, 7680], P(None, 'seq'), may hold values from -0.109375 to 0.109375
- qkv_weight: bfloat16 [1536, 4608], replicated, may hold values from -1 to 1
- out_weight: bfloat16 [1536, 1536], replicated, may hold values from -0.625 to 0.625
- head_weight: bfloat16 [1536, 64], replicated, may hold values from -0.15625 to 0.15625
Outputs:
- guided: float32 [16, 1024, 64], P('seq')
All inputs are finite; a program needn't handle non-finite values.
Results may differ from a plain program's by a relative error of at most 0.0117.
Values may be sent and summed in bfloat16 or wider, within the bound.
A program may use at most 128 MiB of HBM per device.

v0:
```python
import functools
import math

import jax
import jax.numpy as jnp
from jax import lax
from jax.experimental import pallas as pl
from jax.experimental.pallas import tpu as pltpu
from jax.sharding import PartitionSpec as P

HEADS = 24
FREQ = 256
NORM_FLOOR = 0.1
GROUP = 8
VMEM_BYTES = 60 * 1024 * 1024
MESH = pl.DeviceIdType.MESH


def layer_norm(values):
    center = values - jnp.mean(values, axis=-1, keepdims=True)
    spread = jnp.mean(center * center, axis=-1, keepdims=True)
    return center * lax.rsqrt(spread + NORM_FLOOR)


def time_features(timestep):
    half_width = FREQ // 2
    ladder = jnp.arange(half_width, dtype=jnp.float32)
    freq_rates = jnp.exp(-math.log(10000.0) * ladder / half_width)
    angles = timestep.astype(jnp.float32)[0] * freq_rates
    return jnp.concatenate([jnp.cos(angles), jnp.sin(angles)])[None, :].astype(jnp.bfloat16)


def greet_all(n_cfg, n_seq):
    cfg, me = lax.axis_index("cfg"), lax.axis_index("seq")
    barrier = pltpu.get_barrier_semaphore()
    total = n_cfg * n_seq

    def hello(k, carry):
        flat = lax.rem(cfg * n_seq + me + k, total)
        pl.semaphore_signal(
            barrier, inc=1, device_id=(flat // n_seq, lax.rem(flat, n_seq)), device_id_type=MESH
        )
        return carry

    lax.fori_loop(1, total, hello, 0)
    pl.semaphore_wait(barrier, total - 1)


def whole_kernel(
    n_cfg, n_seq, head_dim, scale_ref, ids_ref, placed_ref, latent_ref, table_hbm, mod_w_hbm,
    wqkv_hbm, wo_hbm, wh_hbm, out_ref,
    table, mod_w, wqkv, wo, wh, lat, slots, mods, part, mod_all, normed, qs, ks, vs, mixed, preds,
    load_sem, msg_send, msg_recv, lat_send, lat_recv, mod_send, mod_recv, ret_send, ret_recv,
):
    cfg, me = lax.axis_index("cfg"), lax.axis_index("seq")
    total = n_cfg * n_seq
    mine = cfg * n_seq + me
    frames, pixels, width = latent_ref.shape
    half = pixels // n_cfg
    items = half // n_seq
    groups, all_frames = lat.shape[0], lat.shape[1]
    rows = all_frames * GROUP
    tokens = ids_ref.shape[1]
    voc = table.shape[0]

    loads = []
    for n, (src, dst) in enumerate(
        ((table_hbm, table), (mod_w_hbm, mod_w), (wqkv_hbm, wqkv), (wo_hbm, wo), (wh_hbm, wh))
    ):
        loads.append(pltpu.make_async_copy(src, dst, load_sem.at[n]))
        loads[-1].start()

    def piece(owner, g):
        start = pl.multiple_of(cfg * half + owner * items + g * GROUP, GROUP)
        return latent_ref.at[:, pl.ds(start, GROUP), :]

    def lat_copy(g, k):
        peer = lax.rem(me + k, n_seq)
        return pltpu.make_async_remote_copy(
            src_ref=piece(peer, g), dst_ref=lat.at[g, pl.ds(me * frames, frames)],
            send_sem=lat_send.at[g, k], recv_sem=lat_recv.at[g, k],
            device_id=(cfg, peer), device_id_type=MESH,
        )

    def own_copy(g):
        return pltpu.make_async_copy(
            piece(me, g), lat.at[g, pl.ds(me * frames, frames)], lat_send.at[g, 0]
        )

    def msg_copy(k):
        flat = lax.rem(mine + k, total)
        return pltpu.make_async_remote_copy(
            src_ref=slots.at[mine], dst_ref=slots.at[mine], send_sem=msg_send.at[k],
            recv_sem=msg_recv.at[k],
            device_id=(flat // n_seq, lax.rem(flat, n_seq)), device_id_type=MESH,
        )

    def mod_copy(k):
        peer = lax.rem(me + k, n_seq)
        return pltpu.make_async_remote_copy(
            src_ref=part, dst_ref=mods.at[me], send_sem=mod_send.at[k], recv_sem=mod_recv.at[k],
            device_id=(cfg, peer), device_id_type=MESH,
        )

    def ret_copy(g, k):
        flat = lax.rem(mine + k, total)
        peer = lax.rem(flat, n_seq)
        start = pl.multiple_of(mine * items + g * GROUP, GROUP)
        return pltpu.make_async_remote_copy(
            src_ref=preds.at[g, pl.ds(peer * frames, frames)],
            dst_ref=out_ref.at[:, pl.ds(start, GROUP), :],
            send_sem=ret_send.at[g, k], recv_sem=ret_recv.at[g, k],
            device_id=(flat // n_seq, peer), device_id_type=MESH,
        )

    def own_ret(g):
        start = pl.multiple_of(mine * items + g * GROUP, GROUP)
        return pltpu.make_async_copy(
            preds.at[g, pl.ds(me * frames, frames)],
            out_ref.at[:, pl.ds(start, GROUP), :],
            ret_send.at[g, 0],
        )

    def each(count, act):
        def run(k, carry):
            act(k)
            return carry

        lax.fori_loop(1, count, run, 0)

    greet_all(n_cfg, n_seq)
    own_copy(0).start()
    each(n_seq, lambda k: lat_copy(0, k).start())

    ids = jnp.broadcast_to(ids_ref[...] - me * voc, (128, tokens)).T
    lanes = lax.broadcasted_iota(jnp.int32, (tokens, 128), 1)
    tiles = []
    for t in range(-(-voc // 128)):
        hits = jnp.where(ids == lanes + t * 128, 1.0, 0.0)
        tiles.append(jnp.sum(hits, axis=0, keepdims=True))
    counts = jnp.concatenate(tiles, axis=1)[:, :voc]
    high = jnp.floor(counts * (1.0 / 256.0)) * 256.0
    counts = jnp.concatenate([high, counts - high], axis=0).astype(jnp.bfloat16)
    loads[0].wait()
    sums = jnp.dot(counts, table[...], preferred_element_type=jnp.float32)
    pooled = jnp.sum(sums, axis=0, keepdims=True) * (1.0 / math.sqrt(tokens))
    slots[mine] = pooled + placed_ref[...]
    each(total, lambda k: msg_copy(k).start())
    loads[1].wait()
    each(total, lambda k: msg_copy(k).wait())
    conds = []
    for c in range(n_cfg):
        conds.append(jnp.sum(slots[c * n_seq : (c + 1) * n_seq], axis=0))
    cond = jnp.concatenate(conds, axis=0)
    cond = (cond / (1.0 + jnp.exp(-cond))).astype(jnp.bfloat16)
    mod_part = lax.dot_general(
        cond, mod_w[...], (((1,), (1,)), ((), ())), preferred_element_type=jnp.float32
    )
    part[...] = mod_part
    mods[me] = mod_part
    each(n_seq, lambda k: mod_copy(k).start())
    for g in range(1, groups):
        own_copy(g).start()
        each(n_seq, lambda k: lat_copy(g, k).start())
    each(n_seq, lambda k: mod_copy(k).wait())
    mod_all[...] = jnp.concatenate([mods[s] for s in range(n_seq)], axis=1)
    loads[2].wait()
    loads[3].wait()
    loads[4].wait()

    def modulation(c, n):
        return mod_all[c : c + 1, n * width : (n + 1) * width]

    cols = qs.shape[2]
    steps = width // cols
    pair = 2 * head_dim
    lane = lax.broadcasted_iota(jnp.int32, (1, pair), 1)
    left = jnp.where(lane < head_dim, 1.0, 0.0).astype(jnp.bfloat16)
    right = jnp.where(lane < head_dim, 0.0, 1.0).astype(jnp.bfloat16)
    same = lax.broadcasted_iota(jnp.int32, (1, GROUP, rows), 1) == lax.rem(
        lax.broadcasted_iota(jnp.int32, (1, GROUP, rows), 2), GROUP
    )
    shares = jnp.concatenate(
        [jnp.broadcast_to(left, (rows, pair)), jnp.broadcast_to(right, (rows, pair))], axis=0
    )

    def project(j):
        at = slice(j * cols, (j + 1) * cols)
        x = normed[...]
        q = jnp.dot(x, wqkv[:, at], preferred_element_type=jnp.float32)
        qs[j % 2] = (q * (1.0 / math.sqrt(head_dim))).astype(jnp.bfloat16)
        at = slice(width + j * cols, width + (j + 1) * cols)
        k = jnp.dot(x, wqkv[:, at], preferred_element_type=jnp.float32)
        ks[j % 2] = k.astype(jnp.bfloat16)
        at = slice(2 * width + j * cols, 2 * width + (j + 1) * cols)
        v = jnp.dot(x, wqkv[:, at], preferred_element_type=jnp.float32)
        vs[j % 2] = v.astype(jnp.bfloat16)

    def attend(j, c, h):
        at = slice(c * rows, (c + 1) * rows)
        lanes = slice(h * pair, (h + 1) * pair)
        kk = ks[j % 2, at, lanes]
        vv = vs[j % 2, at, lanes]
        keys = jnp.concatenate([kk * left, kk * right], axis=0)
        vals = jnp.concatenate([vv * left, vv * right], axis=0)
        vals = jnp.concatenate([vals, shares], axis=1)
        scores = lax.dot_general(
            qs[j % 2, at, lanes], keys, (((1,), (1,)), ((), ())),
            preferred_element_type=jnp.float32,
        )
        probs = []
        for s in range(2):
            t = scores[:, s * rows : (s + 1) * rows].reshape(all_frames, GROUP, rows)
            t = jnp.where(same, t, -jnp.inf).reshape(rows, rows)
            e = jnp.exp(t - jnp.max(t, axis=1, keepdims=True))
            probs.append(e.astype(jnp.bfloat16))
        both = jnp.dot(
            jnp.concatenate(probs, axis=1), vals, preferred_element_type=jnp.float32
        )
        o = both[:, :pair] / both[:, pair:]
        start = j * cols + h * pair
        mixed[at, start : start + pair] = o.astype(jnp.bfloat16)

    def wave(g, carry):
        own_copy(g).wait()
        each(n_seq, lambda k: lat_copy(g, k).wait_recv())
        x = lat[g].astype(jnp.float32).reshape(rows, width)
        n = layer_norm(x)
        for c in range(n_cfg):
            y = n * (1.0 + modulation(c, 1)) + modulation(c, 0)
            normed[c * rows : (c + 1) * rows, :] = y.astype(jnp.bfloat16)
        project(0)
        for j in range(steps):
            if j + 1 < steps:
                project(j + 1)
            for c in range(n_cfg):
                for h in range(cols // pair):
                    attend(j, c, h)
        branch = jnp.dot(mixed[...], wo[...], preferred_element_type=jnp.float32)
        x = lat[g].astype(jnp.float32).reshape(rows, width)
        finals = []
        for c in range(n_cfg):
            residual = x + modulation(c, 2) * branch[c * rows : (c + 1) * rows]
            final = layer_norm(residual) * (1.0 + modulation(c, 4)) + modulation(c, 3)
            finals.append(final.astype(jnp.bfloat16))
        both = lax.dot_general(
            jnp.concatenate(finals, axis=0), wh[...], (((1,), (1,)), ((), ())),
            preferred_element_type=jnp.float32,
        )
        guided = both[rows:] + scale_ref[0, 0] * (both[:rows] - both[rows:])
        preds[g] = guided.reshape(all_frames, GROUP, guided.shape[1])
        own_ret(g).start()
        each(total, lambda k: ret_copy(g, k).start())
        return carry

    lax.fori_loop(0, groups, wave, 0)

    def finish(g, carry):
        each(n_seq, lambda k: lat_copy(g, k).wait_send())
        own_ret(g).wait()
        each(total, lambda k: ret_copy(g, k).wait())
        return carry

    lax.fori_loop(0, groups, finish, 0)


def whole(scale, ids, placed, latent, table, mod_weight, qkv_weight, out_weight, head_weight):
    n_cfg, n_seq = lax.axis_size("cfg"), lax.axis_size("seq")
    frames, pixels, width = latent.shape
    head_dim = width // HEADS
    cols = 4 * head_dim
    items = pixels // n_cfg // n_seq
    groups, all_frames = items // GROUP, frames * n_seq
    rows = all_frames * GROUP
    total = n_cfg * n_seq
    mod_cols = mod_weight.shape[0]
    out_ch = head_weight.shape[0]
    vmem = pl.BlockSpec(memory_space=pltpu.VMEM)
    hbm = pl.BlockSpec(memory_space=pl.ANY)
    bf16 = jnp.bfloat16
    dma = pltpu.SemaphoreType.DMA
    return pl.pallas_call(
        functools.partial(whole_kernel, n_cfg, n_seq, head_dim),
        out_shape=jax.ShapeDtypeStruct((frames, pixels, out_ch), jnp.float32),
        in_specs=[
            pl.BlockSpec(memory_space=pltpu.SMEM), vmem, vmem, hbm, hbm, hbm, hbm, hbm, hbm,
        ],
        out_specs=hbm,
        scratch_shapes=[
            pltpu.VMEM(table.shape, bf16),
            pltpu.VMEM(mod_weight.shape, bf16),
            pltpu.VMEM(qkv_weight.shape, bf16),
            pltpu.VMEM(out_weight.shape, bf16),
            pltpu.VMEM(head_weight.shape, bf16),
            pltpu.VMEM((groups, all_frames, GROUP, width), bf16),
            pltpu.VMEM((total, 1, width), jnp.float32),
            pltpu.VMEM((n_seq, n_cfg, mod_cols), jnp.float32),
            pltpu.VMEM((n_cfg, mod_cols), jnp.float32),
            pltpu.VMEM((n_cfg, n_seq * mod_cols), jnp.float32),
            pltpu.VMEM((n_cfg * rows, width), bf16),
            pltpu.VMEM((2, n_cfg * rows, cols), bf16),
            pltpu.VMEM((2, n_cfg * rows, cols), bf16),
            pltpu.VMEM((2, n_cfg * rows, cols), bf16),
            pltpu.VMEM((n_cfg * rows, width), bf16),
            pltpu.VMEM((groups, all_frames, GROUP, out_ch), jnp.float32),
            dma((5,)),
            dma((total,)), dma((total,)),
            dma((groups, n_seq)), dma((groups, n_seq)),
            dma((n_seq,)), dma((n_seq,)),
            dma((groups, total)), dma((groups, total)),
        ],
        compiler_params=pltpu.CompilerParams(
            collective_id=0, has_side_effects=True, vmem_limit_bytes=VMEM_BYTES
        ),
        name="whole",
    )(scale, ids, placed, latent, table, mod_weight, qkv_weight, out_weight, head_weight)


def on_device(
    latent, text_ids, timestep, guide_num, guide_den, text_table,
    time_in, time_out, mod_weight, qkv_weight, out_weight, head_weight,
):
    width = latent.shape[2]
    me = lax.axis_index("seq")
    time_hidden = jax.nn.silu(
        jnp.dot(time_features(timestep), time_in, preferred_element_type=jnp.float32)
    ).astype(jnp.bfloat16)
    time_part = jnp.dot(time_hidden, time_out, preferred_element_type=jnp.float32)
    placed = lax.dynamic_update_slice(
        jnp.zeros((1, width), jnp.float32), time_part, (0, me * time_out.shape[1])
    )
    guide_scale = guide_num[0].astype(jnp.float32) / guide_den[0].astype(jnp.float32)
    return whole(
        guide_scale.reshape(1, 1), text_ids, placed, latent, text_table, mod_weight.T,
        qkv_weight, out_weight, head_weight.T,
    )


def solution(mesh):
    in_specs = (
        P("seq", None, None), P("cfg", None), P(), P(), P(), P("seq", None),
        P(), P(None, "seq"), P(None, "seq"), P(), P(), P(),
    )
    return jax.shard_map(
        on_device, mesh=mesh, in_specs=in_specs, out_specs=P("seq", None, None), check_vma=False
    )
```

profile of v0, /device:TPU:0, one launch (start us, length us, event | category | flops | bytes accessed | tf_op | source)
XLA Modules:
  0.0 83.8 jit_solution(5616013452446826188)
XLA Ops:
  0.0 0.0 copy-start
  2.1 0.1 sine_convert_fusion
  2.1 0.0 copy-done
  2.2 0.2 convolution_reduce_fusion
  2.4 1.1 %fusion = f32[1,96]{1,0:T(1,128)S(1)} fusion(bf16[1536,1]{0,1:T(2,128)(2,1)S(1)} %reshape.28, bf16[1536,96]{0,1:T(8,128)(2,1)} %param.19), kind=kOutput, calls=%fused_computation.6 | convolution fusion | flops 294912 | bytes 298368 | tf_op jit(solution)/shard_map/dot_general | solution.py:328
  3.5 0.1 dynamic_update_slice.3.placed_ref
  3.7 0.0 copy-start.1
  3.7 0.6 copy-done.1
  4.3 77.6 %whole.1 = f32[1,1024,64]{2,1,0:T(8,128)} custom-call(f32[1,1]{1,0:T(1,128)} %bitcast.scale_ref, s32[1,512]{1,0:T(1,128)} %ids_ref.1, f32[1,1536]{1,0:T(1,128)} %copy-done.1, bf16[1,1024,1536]{2,1,0:T(8,128)(2,1)} %latent_ref.1, bf16[2008,1536]{1,0:T(8,128)(2,1)} %table_hbm.1, bf16[480,1536]{1,0:T(8,128)(2,1)} %bitcast.9, bf16[1536,4608]{1,0:T(8,128)(2,1)} %wqkv_hbm.1, ...), custom_call_target="tpu_custom_call" | custom-call | tf_op jit(solution)/shard_map/whole/pallas_call | solution.py:282
  81.9 1.9 %copy.13 = f32[1,1024,64]{1,2,0:T(8,128)} copy(f32[1,1024,64]{2,1,0:T(8,128)} %whole.1) | data formatting | bytes 524288 | tf_op jit(solution)/shard_map/whole/pallas_call | solution.py:282
  (5 shorter events, 0.0 us)
Async XLA Ops:
  0.0 2.1 %copy-start = (bf16[256,1536]{1,0:T(8,128)(2,1)S(1)}, bf16[256,1536]{1,0:T(8,128)(2,1)}, u32[]{:S(2)}) copy-start(bf16[256,1536]{1,0:T(8,128)(2,1)} %param.18) | copy-start | bytes 2359300
  3.7 0.6 copy-start.1
where the time goes:
time: 84.1 us; the launch traced here: 83.8 us
  Pallas kernels  77.6 us (92%)
  local copies, waits for them, and re-layouts  2.67 us (3%)
  between operations  2.13 us (3%)
  matrix products  1.33 us (2%)
    pallas_call x1, Pallas kernels, whole(): pl.pallas_call(functools.partial(whole_kernel, n_cfg, n_seq, head_dim), o...  77.6 us
    pallas_call x1, local copies, waits for them, and re-layouts, whole(): pl.pallas_call(functools.partial(whole_kernel, n_cfg, n_seq, head_dim), o...  1.93 us

commit v1 on v0

v1 whole, which is shorter than its diff:
```python
import functools
import math

import jax
import jax.numpy as jnp
from jax import lax
from jax.experimental import pallas as pl
from jax.experimental.pallas import tpu as pltpu
from jax.sharding import PartitionSpec as P

HEADS = 24
FREQ = 256
NORM_FLOOR = 0.1
GROUP = 8
PACK = 2
BATCH = 2
FIRST_FAR = 2
SECOND_FAR = 6
VMEM_BYTES = 60 * 1024 * 1024
MESH = pl.DeviceIdType.MESH


def layer_norm(values):
    center = values - jnp.mean(values, axis=-1, keepdims=True)
    spread = jnp.mean(center * center, axis=-1, keepdims=True)
    return center * lax.rsqrt(spread + NORM_FLOOR)


def silu(values):
    return values / (1.0 + jnp.exp(-values))


def each(low, high, act):
    def run(k, carry):
        act(k)
        return carry

    lax.fori_loop(low, high, run, 0)


def whole_kernel(
    n_cfg, n_seq, head_dim, step_ref, num_ref, den_ref, ids_ref, latent_ref, table_hbm, tin_hbm,
    tout_hbm, mod_w_hbm, wqkv_hbm, wo_hbm, wh_hbm, out_ref,
    table, tin, tout, mod_w, wqkv, wo, wh, lat, slots, mods, mod_all, normed, qkv, mixed, preds,
    landed, load_sem, msg_send, msg_recv, near_send, near_recv, far_send, far_recv, mod_send,
    mod_recv, ret_send, ret_recv,
):
    cfg, me = lax.axis_index("cfg"), lax.axis_index("seq")
    total = n_cfg * n_seq
    mine = cfg * n_seq + me
    half_seq = n_seq // 2
    side, spot = me // half_seq, lax.rem(me, half_seq)
    frames, pixels, width = latent_ref.shape
    items = pixels // n_cfg // n_seq
    groups, all_frames = lat.shape[0], lat.shape[1]
    rows = all_frames * GROUP
    part_rows = rows // 2
    part_frames = all_frames // 2
    tokens = ids_ref.shape[1]
    voc = table.shape[0]
    out_ch = wh.shape[0] // PACK
    pairs = preds.shape[0]

    loads = []
    for n, (src, dst) in enumerate(
        (
            (table_hbm, table), (tin_hbm, tin), (tout_hbm, tout), (mod_w_hbm, mod_w),
            (wqkv_hbm, wqkv), (wo_hbm, wo), (wh_hbm, wh.at[:out_ch]), (wh_hbm, wh.at[out_ch:]),
        )
    ):
        loads.append(pltpu.make_async_copy(src, dst, load_sem.at[n]))
    for n in range(4):
        loads[n].start()

    def device(flat):
        return (flat // n_seq, lax.rem(flat, n_seq))

    barrier = pltpu.get_barrier_semaphore()
    each(1, total, lambda k: pl.semaphore_signal(
        barrier, inc=1, device_id=device(lax.rem(mine + k, total)), device_id_type=MESH
    ))

    def piece(owner, g):
        start = pl.multiple_of(cfg * (pixels // n_cfg) + owner * items + g * GROUP, GROUP)
        return latent_ref.at[:, pl.ds(start, GROUP), :]

    def place(source, at_side):
        return lax.rem(source + n_seq - at_side * half_seq, n_seq) * frames

    def near_copy(g, k):
        peer = side * half_seq + lax.rem(spot + k, half_seq)
        return pltpu.make_async_remote_copy(
            src_ref=piece(peer, g), dst_ref=lat.at[g, pl.ds(place(me, side), frames)],
            send_sem=near_send.at[g, k], recv_sem=near_recv.at[g, k],
            device_id=(cfg, peer), device_id_type=MESH,
        )

    def far_copy(g, k):
        peer = (1 - side) * half_seq + lax.rem(spot + k, half_seq)
        return pltpu.make_async_remote_copy(
            src_ref=piece(peer, g), dst_ref=lat.at[g, pl.ds(place(me, 1 - side), frames)],
            send_sem=far_send.at[g, k], recv_sem=far_recv.at[g, k],
            device_id=(cfg, peer), device_id_type=MESH,
        )

    def own_copy(g):
        return pltpu.make_async_copy(
            piece(me, g), lat.at[g, pl.ds(place(me, side), frames)], near_send.at[g, 0]
        )

    def msg_copy(k):
        peer = lax.rem(me + k, n_seq)
        return pltpu.make_async_remote_copy(
            src_ref=slots.at[me], dst_ref=slots.at[me], send_sem=msg_send.at[k],
            recv_sem=msg_recv.at[k], device_id=(cfg, peer), device_id_type=MESH,
        )

    def mod_copy(k):
        return pltpu.make_async_remote_copy(
            src_ref=mods.at[mine], dst_ref=mods.at[mine], send_sem=mod_send.at[k],
            recv_sem=mod_recv.at[k], device_id=device(lax.rem(mine + k, total)),
            device_id_type=MESH,
        )

    def ret_copy(q, k):
        flat = lax.rem(mine + k, total)
        return pltpu.make_async_remote_copy(
            src_ref=preds.at[q, pl.ds(place(lax.rem(flat, n_seq), side), frames)],
            dst_ref=landed.at[q, mine], send_sem=ret_send.at[q, k], recv_sem=ret_recv.at[q, k],
            device_id=device(flat), device_id_type=MESH,
        )

    ids = jnp.broadcast_to(ids_ref[...] - me * voc, (128, tokens)).T
    lanes = lax.broadcasted_iota(jnp.int32, (tokens, 128), 1)
    tiles = []
    for t in range(-(-voc // 128)):
        hits = jnp.where(ids == lanes + t * 128, 1.0, 0.0)
        tiles.append(jnp.sum(hits, axis=0, keepdims=True))
    counts = jnp.concatenate(tiles, axis=1)[:, :voc]
    high = jnp.floor(counts * (1.0 / 256.0)) * 256.0
    counts = jnp.concatenate([high, counts - high], axis=0).astype(jnp.bfloat16)

    pl.semaphore_wait(barrier, total - 1)
    each(0, FIRST_FAR, lambda k: far_copy(0, k).start())
    own_copy(0).start()
    each(1, half_seq, lambda k: near_copy(0, k).start())

    time = jnp.full((1, FREQ // 2), step_ref[0], jnp.int32).astype(jnp.float32)
    ladder = lax.broadcasted_iota(jnp.int32, (1, FREQ // 2), 1).astype(jnp.float32)
    angles = time * jnp.exp(-math.log(10000.0) * ladder / (FREQ // 2))
    time_freq = jnp.concatenate([jnp.cos(angles), jnp.sin(angles)], axis=1).astype(jnp.bfloat16)
    loads[1].wait()
    hidden = silu(jnp.dot(time_freq, tin[...], preferred_element_type=jnp.float32))
    loads[2].wait()
    time_part = lax.dot_general(
        hidden.astype(jnp.bfloat16), tout[...], (((1,), (1,)), ((), ())),
        preferred_element_type=jnp.float32,
    )
    lane = lax.broadcasted_iota(jnp.int32, (1, width), 1)
    first = me * tout.shape[0]
    placed = jnp.where(
        (lane >= first) & (lane < first + tout.shape[0]),
        jnp.concatenate([time_part] * n_seq, axis=1), 0.0,
    )

    loads[0].wait()
    for n in range(4, 8):
        loads[n].start()
    sums = jnp.dot(counts, table[...], preferred_element_type=jnp.float32)
    pooled = jnp.sum(sums, axis=0, keepdims=True) * (1.0 / math.sqrt(tokens))
    slots[me] = pooled + placed
    each(1, n_seq, lambda k: msg_copy(k).start())
    each(FIRST_FAR, SECOND_FAR, lambda k: far_copy(0, k).start())
    for g in range(1, min(2, groups)):
        own_copy(g).start()
        each(1, half_seq, lambda k: near_copy(g, k).start())
    loads[3].wait()
    each(1, n_seq, lambda k: msg_copy(k).wait())
    cond = silu(jnp.sum(slots[...], axis=0)).astype(jnp.bfloat16)
    mods[mine] = lax.dot_general(
        cond, mod_w[...], (((1,), (1,)), ((), ())), preferred_element_type=jnp.float32
    )
    each(1, total, lambda k: mod_copy(k).start())
    each(SECOND_FAR, half_seq, lambda k: far_copy(0, k).start())
    for g in range(2, groups):
        own_copy(g).start()
        each(1, half_seq, lambda k: near_copy(g, k).start())
    for g in range(1, groups):
        each(0, half_seq, lambda k: far_copy(g, k).start())
    each(1, total, lambda k: mod_copy(k).wait())
    for c in range(n_cfg):
        mod_all[c : c + 1] = jnp.concatenate(
            [mods[c * n_seq + s] for s in range(n_seq)], axis=1
        )
    for n in range(4, 8):
        loads[n].wait()

    def modulation(c, n):
        return mod_all[c : c + 1, n * width : (n + 1) * width]

    def modulated(g, where, at):
        x = lat[g, where].astype(jnp.float32).reshape(part_rows, width)
        n = layer_norm(x)
        for c in range(n_cfg):
            y = n * (1.0 + modulation(c, 1)) + modulation(c, 0)
            start = at + c * part_rows
            normed[start : start + part_rows, :] = y.astype(jnp.bfloat16)

    chunk = 4 * head_dim
    steps = width // chunk

    def project(x, j, part):
        at = slice(part * width + j * chunk, part * width + (j + 1) * chunk)
        out = jnp.dot(x, wqkv[:, at], preferred_element_type=jnp.float32)
        if part == 0:
            out = out * (1.0 / math.sqrt(head_dim))
        return at, out.astype(jnp.bfloat16)

    batch = min(BATCH, groups)

    def near_wave(b, carry):
        for n in range(batch):
            g = b * batch + n
            own_copy(g).wait()
            each(1, half_seq, lambda k: near_copy(g, k).wait_recv())
        for n in range(batch):
            modulated(b * batch + n, slice(0, part_frames), n * n_cfg * part_rows)
        x = normed[...]
        for j in range(steps):
            for part in range(3):
                at, out = project(x, j, part)
                for n in range(batch):
                    for c in range(n_cfg):
                        start = (n * n_cfg + c) * part_rows
                        qkv[b * batch + n, c, :part_rows, at] = out[start : start + part_rows]
        return carry

    lax.fori_loop(0, groups // batch, near_wave, 0)

    pair = 2 * head_dim
    lane = lax.broadcasted_iota(jnp.int32, (1, pair), 1)
    left = jnp.where(lane < head_dim, 1.0, 0.0).astype(jnp.bfloat16)
    right = jnp.where(lane < head_dim, 0.0, 1.0).astype(jnp.bfloat16)
    same = lax.broadcasted_iota(jnp.int32, (1, GROUP, rows), 1) == lax.rem(
        lax.broadcasted_iota(jnp.int32, (1, GROUP, rows), 2), GROUP
    )
    shares = jnp.concatenate(
        [jnp.broadcast_to(left, (rows, pair)), jnp.broadcast_to(right, (rows, pair))], axis=0
    )
    top = jnp.full((1, PACK * out_ch), num_ref[0], jnp.int32).astype(jnp.float32)
    bottom = jnp.full((1, PACK * out_ch), den_ref[0], jnp.int32).astype(jnp.float32)
    guide_scale = top / bottom

    def attend(g, c, start):
        q = qkv[g, c, :, start : start + pair]
        kk = qkv[g, c, :, width + start : width + start + pair]
        vv = qkv[g, c, :, 2 * width + start : 2 * width + start + pair]
        keys = jnp.concatenate([kk * left, kk * right], axis=0)
        vals = jnp.concatenate([vv * left, vv * right], axis=0)
        vals = jnp.concatenate([vals, shares], axis=1)
        scores = lax.dot_general(
            q, keys, (((1,), (1,)), ((), ())), preferred_element_type=jnp.float32
        )
        probs = []
        for s in range(2):
            t = scores[:, s * rows : (s + 1) * rows].reshape(all_frames, GROUP, rows)
            t = jnp.where(same, t, -jnp.inf).reshape(rows, rows)
            e = jnp.exp(t - jnp.max(t, axis=1, keepdims=True))
            probs.append(e.astype(jnp.bfloat16))
        both = jnp.dot(
            jnp.concatenate(probs, axis=1), vals, preferred_element_type=jnp.float32
        )
        o = both[:, :pair] / both[:, pair:]
        mixed[c * rows : (c + 1) * rows, start : start + pair] = o.astype(jnp.bfloat16)

    def far_wave(g, carry):
        each(0, half_seq, lambda k: far_copy(g, k).wait_recv())
        modulated(g, slice(part_frames, all_frames), 0)
        x = normed[: n_cfg * part_rows]

        def extend(j):
            for part in range(3):
                at, out = project(x, j, part)
                for c in range(n_cfg):
                    qkv[g, c, part_rows:, at] = out[c * part_rows : (c + 1) * part_rows]

        extend(0)
        for j in range(steps):
            if j + 1 < steps:
                extend(j + 1)
            for c in range(n_cfg):
                for h in range(chunk // pair):
                    attend(g, c, j * chunk + h * pair)
        branch = jnp.dot(mixed[...], wo[...], preferred_element_type=jnp.float32)
        x = lat[g].astype(jnp.float32).reshape(rows, width)
        finals = []
        for c in range(n_cfg):
            residual = x + modulation(c, 2) * branch[c * rows : (c + 1) * rows]
            final = layer_norm(residual) * (1.0 + modulation(c, 4)) + modulation(c, 3)
            finals.append(final.astype(jnp.bfloat16))
        both = lax.dot_general(
            jnp.concatenate(finals, axis=0), wh[...], (((1,), (1,)), ((), ())),
            preferred_element_type=jnp.float32,
        )
        guided = both[rows:] + guide_scale * (both[:rows] - both[rows:])
        guided = guided.reshape(all_frames, GROUP, PACK * out_ch).astype(preds.dtype)
        q = g // PACK

        @pl.when(lax.rem(g, PACK) == 0)
        def _():
            preds[q] = guided

        @pl.when(lax.rem(g, PACK) != 0)
        def _():
            preds[q, :, :, out_ch:] = guided[:, :, out_ch:]

        @pl.when((lax.rem(g, PACK) == PACK - 1) | (g == groups - 1))
        def _():
            each(1, total, lambda k: ret_copy(q, k).start())
            landed[q, mine] = preds[q, pl.ds(place(me, side), frames)]

        return carry

    lax.fori_loop(0, groups, far_wave, 0)

    for g in range(groups):
        each(1, half_seq, lambda k: near_copy(g, k).wait_send())
        each(0, half_seq, lambda k: far_copy(g, k).wait_send())
    for q in range(pairs):
        each(1, total, lambda k: ret_copy(q, k).wait())
    for f in range(frames):
        slabs = []
        for source in range(total):
            for g in range(groups):
                slab = landed[g // PACK, source, f].astype(jnp.float32)
                if g % PACK:
                    slab = pltpu.roll(slab, out_ch, 1)
                slabs.append(slab)
        per = 128 // GROUP
        for n in range(pixels // 128):
            block = jnp.concatenate(slabs[n * per : (n + 1) * per], axis=0)
            out_ref[f, :, n * 128 : (n + 1) * 128] = block.T[:out_ch]


def whole(step, num, den, ids, latent, table, tin, tout, mod_w, wqkv, wo, wh):
    n_cfg, n_seq = lax.axis_size("cfg"), lax.axis_size("seq")
    frames, pixels, width = latent.shape
    head_dim = width // HEADS
    items = pixels // n_cfg // n_seq
    groups, all_frames = items // GROUP, frames * n_seq
    rows = all_frames * GROUP
    total = n_cfg * n_seq
    half_seq = n_seq // 2
    batch = min(BATCH, groups)
    pairs = -(-groups // PACK)
    mod_cols = mod_w.shape[0]
    out_ch = wh.shape[0]
    smem = pl.BlockSpec(memory_space=pltpu.SMEM)
    vmem = pl.BlockSpec(memory_space=pltpu.VMEM)
    hbm = pl.BlockSpec(memory_space=pl.ANY)
    bf16 = jnp.bfloat16
    dma = pltpu.SemaphoreType.DMA
    return pl.pallas_call(
        functools.partial(whole_kernel, n_cfg, n_seq, head_dim),
        out_shape=jax.ShapeDtypeStruct((frames, out_ch, pixels), jnp.float32),
        in_specs=[smem, smem, smem, vmem, hbm, hbm, hbm, hbm, hbm, hbm, hbm, hbm],
        out_specs=vmem,
        scratch_shapes=[
            pltpu.VMEM(table.shape, bf16),
            pltpu.VMEM(tin.shape, bf16),
            pltpu.VMEM(tout.shape, bf16),
            pltpu.VMEM(mod_w.shape, bf16),
            pltpu.VMEM(wqkv.shape, bf16),
            pltpu.VMEM(wo.shape, bf16),
            pltpu.VMEM((PACK * out_ch, width), bf16),
            pltpu.VMEM((groups, all_frames, GROUP, width), bf16),
            pltpu.VMEM((n_seq, 1, width), jnp.float32),
            pltpu.VMEM((total, 1, mod_cols), jnp.float32),
            pltpu.VMEM((n_cfg, n_seq * mod_cols), jnp.float32),
            pltpu.VMEM((batch * n_cfg * rows // 2, width), bf16),
            pltpu.VMEM((groups, n_cfg, rows, 3 * width), bf16),
            pltpu.VMEM((n_cfg * rows, width), bf16),
            pltpu.VMEM((pairs, all_frames, GROUP, PACK * out_ch), bf16),
            pltpu.VMEM((pairs, total, frames, GROUP, PACK * out_ch), bf16),
            dma((8,)),
            dma((n_seq,)), dma((n_seq,)),
            dma((groups, half_seq)), dma((groups, half_seq)),
            dma((groups, half_seq)), dma((groups, half_seq)),
            dma((total,)), dma((total,)),
            dma((pairs, total)), dma((pairs, total)),
        ],
        compiler_params=pltpu.CompilerParams(
            collective_id=0, has_side_effects=True, vmem_limit_bytes=VMEM_BYTES
        ),
        name="whole",
    )(step, num, den, ids, latent, table, tin, tout, mod_w, wqkv, wo, wh)


def on_device(
    latent, text_ids, timestep, guide_num, guide_den, text_table,
    time_in, time_out, mod_weight, qkv_weight, out_weight, head_weight,
):
    out = whole(
        timestep, guide_num, guide_den, text_ids, latent, text_table, time_in, time_out.T,
        mod_weight.T, qkv_weight, out_weight, head_weight.T,
    )
    return jnp.swapaxes(out, 1, 2)


def solution(mesh):
    in_specs = (
        P("seq", None, None), P("cfg", None), P(), P(), P(), P("seq", None),
        P(), P(None, "seq"), P(None, "seq"), P(), P(), P(),
    )
    return jax.shard_map(
        on_device, mesh=mesh, in_specs=in_specs, out_specs=P("seq", None, None), check_vma=False
    )
```

time: 84.1 us -> 74.7 us (0.89)
  Pallas kernels: 77.6 us -> 70.9 us
  matrix products: 1.33 us -> 0 us
  local copies, waits for them, and re-layouts: 2.67 us -> 1.67 us
    pallas_call x1, Pallas kernels: 77.6 us -> 70.9 us  [whole(): pl.pallas_call(functools.partial(whole_kernel, n_cfg, n_seq, head_dim), o...]
    pallas_call x1 -> x0, local copies, waits for them, and re-layouts: 1.93 us -> none  [whole(): pl.pallas_call(functools.partial(whole_kernel, n_cfg, n_seq, head_dim), o...]
    dot_general x2 -> x0, matrix products: 1.33 us -> none  [the longest x1 1.12 us: on_device(): jnp.dot(time_hidden, time_out, preferred_element_type=jnp.float32)]
    unnamed x4 -> x1, local copies, waits for them, and re-layouts: 0.59 us -> 1.67 us
where the time goes in v1:
time: 74.7 us; the launch traced here: 74.5 us
  Pallas kernels  70.9 us (95%)
  between operations  1.95 us (3%)
  local copies, waits for them, and re-layouts  1.67 us (2%)
    pallas_call x1, Pallas kernels, whole(): pl.pallas_call(functools.partial(whole_kernel, n_cfg, n_seq, head_dim), o...  70.9 us
    unnamed x1, local copies, waits for them, and re-layouts  1.67 us

profile of v1, /device:TPU:0, one launch (start us, length us, event | category | flops | bytes accessed | tf_op | source)
XLA Modules:
  0.0 74.5 jit_solution(4751959469642172087)
XLA Ops:
  1.9 70.9 %whole.1 = f32[1,64,1024]{2,1,0:T(8,128)} custom-call(s32[1]{0:T(128)S(6)} %copy.14.step_ref, s32[1]{0:T(128)S(6)} %copy.15.num_ref, s32[1]{0:T(128)S(6)} %copy.16.den_ref, s32[1,512]{1,0:T(1,128)} %ids_ref.1, bf16[1,1024,1536]{2,1,0:T(8,128)(2,1)} %latent_ref.1, bf16[2008,1536]{1,0:T(8,128)(2,1)} %table_hbm.1, bf16[256,1536]{1,0:T(8,128)(2,1)} %tin_hbm.1, ...), custom_call_target="tpu_custom_call" | custom-call | tf_op jit(solution)/shard_map/whole/pallas_call | solution.py:363
  72.8 1.7 %copy.17 = f32[1,1024,64]{1,2,0:T(8,128)} copy(f32[1,1024,64]{1,2,0:T(8,128)} %bitcast.5) | data formatting | bytes 524288

commit v2 on v1

v2 whole, which is shorter than its diff:
```python
import functools
import math

import jax
import jax.numpy as jnp
from jax import lax
from jax.experimental import pallas as pl
from jax.experimental.pallas import tpu as pltpu
from jax.sharding import PartitionSpec as P

HEADS = 24
FREQ = 256
NORM_FLOOR = 0.1
GROUP = 8
PACK = 2
EDGE_EARLY = 5
MIDDLE_EARLY = 8
AHEAD = 2
NEAR_EARLY = 2
SLICE = 512
VMEM_BYTES = 60 * 1024 * 1024
MESH = pl.DeviceIdType.MESH


def layer_norm(values):
    center = values - jnp.mean(values, axis=-1, keepdims=True)
    spread = jnp.mean(center * center, axis=-1, keepdims=True)
    return center * lax.rsqrt(spread + NORM_FLOOR)


def silu(values):
    return values / (1.0 + jnp.exp(-values))


def each(low, high, act):
    def run(k, carry):
        act(k)
        return carry

    lax.fori_loop(low, high, run, 0)


def whole_kernel(
    n_cfg, n_seq, head_dim, step_hbm, num_hbm, den_hbm, ids_hbm, latent_ref, table_hbm, tin_hbm,
    tout_hbm, mod_w_hbm, wqkv_hbm, wo_hbm, wh_hbm, out_ref,
    step, num, den, ids_ref, table, tin, tout, mod_w, wqkv, wo, wh, lat, slots, mods, mod_all,
    normed, qkv, mixed, branch, finals, spare, preds, landed, load_sem, msg_sem, mod_sem, own_sem,
    lat_sem, ret_send, ret_recv,
):
    cfg, me = lax.axis_index("cfg"), lax.axis_index("seq")
    total = n_cfg * n_seq
    mine = cfg * n_seq + me
    half_seq = n_seq // 2
    side, spot = me // half_seq, lax.rem(me, half_seq)
    edge = jnp.where((2 * me // half_seq == 0) | (2 * me // half_seq == 3), 1, 0)
    early = min(MIDDLE_EARLY, half_seq) + edge * (min(EDGE_EARLY, half_seq) - min(MIDDLE_EARLY, half_seq))
    frames, pixels, width = latent_ref.shape
    items = pixels // n_cfg // n_seq
    groups, all_frames = lat.shape[0], lat.shape[1]
    rows = all_frames * GROUP
    part_rows, part_frames = rows // 2, all_frames // 2
    tokens = ids_ref.shape[1]
    voc = table.shape[0]
    out_ch = wh.shape[0] // PACK
    pairs = preds.shape[0]
    batch = normed.shape[0] // rows * 2 // n_cfg

    loads = []
    for n, (src, dst) in enumerate(
        (
            (ids_hbm, ids_ref), (step_hbm, step), (tin_hbm, tin), (tout_hbm, tout),
            (mod_w_hbm, mod_w), (num_hbm, num), (den_hbm, den),
            (wqkv_hbm, wqkv), (wo_hbm, wo), (wh_hbm, wh.at[:out_ch]), (wh_hbm, wh.at[out_ch:]),
        )
    ):
        loads.append(pltpu.make_async_copy(src, dst, load_sem.at[n]))
    cuts = list(range(0, voc, SLICE)) + [voc]
    strips = []
    for n, (low, high) in enumerate(zip(cuts[:-1], cuts[1:])):
        strip = slice(low, high)
        strips.append((strip, pltpu.make_async_copy(
            table_hbm.at[strip], table.at[strip], load_sem.at[len(loads) + n]
        )))
    loads[0].start()
    loads[1].start()
    loads[2].start()
    strips[0][1].start()
    loads[3].start()
    for _, strip_copy in strips[1:]:
        strip_copy.start()

    def device(flat):
        return (flat // n_seq, lax.rem(flat, n_seq))

    barrier = pltpu.get_barrier_semaphore()
    each(1, total, lambda k: pl.semaphore_signal(
        barrier, inc=1, device_id=device(lax.rem(mine + k, total)), device_id_type=MESH
    ))

    def piece(owner, g):
        start = pl.multiple_of(cfg * (pixels // n_cfg) + owner * items + g * GROUP, GROUP)
        return latent_ref.at[:, pl.ds(start, GROUP), :]

    def place(source, at_side):
        return lax.rem(source + n_seq - at_side * half_seq, n_seq) * frames

    def near_copy(g, k):
        peer = side * half_seq + lax.rem(spot + k, half_seq)
        return pltpu.make_async_remote_copy(
            src_ref=piece(peer, g), dst_ref=lat.at[g, pl.ds(place(me, side), frames)],
            send_sem=lat_sem.at[2 * groups], recv_sem=lat_sem.at[g],
            device_id=(cfg, peer), device_id_type=MESH,
        )

    def far_copy(g, k):
        peer = (1 - side) * half_seq + lax.rem(spot + k, half_seq)
        return pltpu.make_async_remote_copy(
            src_ref=piece(peer, g), dst_ref=lat.at[g, pl.ds(place(me, 1 - side), frames)],
            send_sem=lat_sem.at[2 * groups], recv_sem=lat_sem.at[groups + g],
            device_id=(cfg, peer), device_id_type=MESH,
        )

    def own_copy(g):
        return pltpu.make_async_copy(
            piece(me, g), lat.at[g, pl.ds(place(me, side), frames)], own_sem.at[g]
        )

    def send_near(g):
        own_copy(g).start()
        each(1, half_seq, lambda k: near_copy(g, k).start())

    def send_far(g, low, high):
        each(low, high, lambda k: far_copy(g, k).start())

    def msg_copy(k):
        peer = lax.rem(me + k, n_seq)
        return pltpu.make_async_remote_copy(
            src_ref=slots.at[me], dst_ref=slots.at[me], send_sem=msg_sem.at[0],
            recv_sem=msg_sem.at[1], device_id=(cfg, peer), device_id_type=MESH,
        )

    def mod_copy(k):
        return pltpu.make_async_remote_copy(
            src_ref=mods.at[mine], dst_ref=mods.at[mine], send_sem=mod_sem.at[0],
            recv_sem=mod_sem.at[1], device_id=device(lax.rem(mine + k, total)),
            device_id_type=MESH,
        )

    def ret_copy(q, k):
        flat = lax.rem(mine + k, total)
        return pltpu.make_async_remote_copy(
            src_ref=preds.at[q, pl.ds(place(lax.rem(flat, n_seq), side), frames)],
            dst_ref=landed.at[q, mine], send_sem=ret_send.at[q], recv_sem=ret_recv.at[q],
            device_id=device(flat), device_id_type=MESH,
        )

    def drain(ref, sem):
        pltpu.make_async_copy(ref, ref, sem).wait()
    loads[0].wait()
    ids = jnp.broadcast_to(ids_ref[...] - me * voc, (128, tokens)).T
    lanes = lax.broadcasted_iota(jnp.int32, (tokens, 128), 1)
    tiles = []
    for t in range(-(-voc // 128)):
        hits = jnp.where(ids == lanes + t * 128, 1.0, 0.0)
        tiles.append(jnp.sum(hits, axis=0, keepdims=True))
    counts = jnp.concatenate(tiles, axis=1)[:, :voc]
    high = jnp.floor(counts * (1.0 / 256.0)) * 256.0
    counts = jnp.concatenate([high, counts - high], axis=0).astype(jnp.bfloat16)
    loads[1].wait()
    time = jnp.full((1, FREQ // 2), step[0], jnp.int32).astype(jnp.float32)
    ladder = lax.broadcasted_iota(jnp.int32, (1, FREQ // 2), 1).astype(jnp.float32)
    angles = time * jnp.exp(-math.log(10000.0) * ladder / (FREQ // 2))
    time_freq = jnp.concatenate([jnp.cos(angles), jnp.sin(angles)], axis=1).astype(jnp.bfloat16)
    loads[2].wait()
    hidden = silu(jnp.dot(time_freq, tin[...], preferred_element_type=jnp.float32))
    loads[3].wait()
    time_part = lax.dot_general(
        hidden.astype(jnp.bfloat16), tout[...], (((1,), (1,)), ((), ())),
        preferred_element_type=jnp.float32,
    )
    lane = lax.broadcasted_iota(jnp.int32, (1, width), 1)
    first = me * tout.shape[0]
    placed = jnp.where(
        (lane >= first) & (lane < first + tout.shape[0]),
        jnp.concatenate([time_part] * n_seq, axis=1), 0.0,
    )
    sums = jnp.zeros((2, width), jnp.float32)
    for strip, strip_copy in strips:
        strip_copy.wait()
        sums += jnp.dot(counts[:, strip], table[strip, :], preferred_element_type=jnp.float32)
    for n in range(4, 11):
        loads[n].start()
    pooled = jnp.sum(sums, axis=0, keepdims=True) * (1.0 / math.sqrt(tokens)) + placed
    wide = width // 2
    slots[me] = jnp.concatenate([pooled[:, :wide], pooled[:, wide:]], axis=0).astype(slots.dtype)
    pl.semaphore_wait(barrier, total - 1)
    each(1, n_seq, lambda k: msg_copy(k).start())
    for g in range(min(NEAR_EARLY, groups)):
        send_near(g)
    send_far(0, 0, early)
    loads[4].wait()
    drain(slots.at[pl.ds(0, n_seq - 1)], msg_sem.at[1])
    cond = silu(jnp.sum(slots[...].astype(jnp.float32), axis=0)).astype(jnp.bfloat16)
    cond = jnp.concatenate([cond[:1], cond[1:]], axis=1)
    mods[mine] = lax.dot_general(
        cond, mod_w[...], (((1,), (1,)), ((), ())), preferred_element_type=jnp.float32
    )
    each(1, total, lambda k: mod_copy(k).start())
    for g in range(min(NEAR_EARLY, groups), groups):
        send_near(g)
    send_far(0, early, half_seq)
    for g in range(1, groups):
        send_far(g, 0, half_seq if g < AHEAD else half_seq * edge)
    for n in range(5, 11):
        loads[n].wait()
    drain(mods.at[pl.ds(0, total - 1)], mod_sem.at[1])
    for c in range(n_cfg):
        mod_all[c : c + 1] = jnp.concatenate(
            [mods[c * n_seq + s] for s in range(n_seq)], axis=1
        )

    def modulation(c, n):
        return mod_all[c : c + 1, n * width : (n + 1) * width]

    chunk = 4 * head_dim
    steps = width // chunk
    pair = 2 * head_dim
    slab = rows // 4
    slab_frames = all_frames // 4
    lane = lax.broadcasted_iota(jnp.int32, (1, pair), 1)
    left = jnp.where(lane < head_dim, 1.0, 0.0).astype(jnp.bfloat16)
    right = jnp.where(lane < head_dim, 0.0, 1.0).astype(jnp.bfloat16)
    same = lax.broadcasted_iota(jnp.int32, (1, GROUP, rows), 1) == lax.rem(
        lax.broadcasted_iota(jnp.int32, (1, GROUP, rows), 2), GROUP
    )
    shares = jnp.concatenate(
        [jnp.broadcast_to(left, (rows, pair)), jnp.broadcast_to(right, (rows, pair))], axis=0
    )
    top = jnp.full((1, PACK * out_ch), num[0], jnp.int32).astype(jnp.float32)
    bottom = jnp.full((1, PACK * out_ch), den[0], jnp.int32).astype(jnp.float32)
    guide_scale = top / bottom

    def near_arrive(g):
        own_copy(g).wait()
        drain(lat.at[g, pl.ds(0, part_frames - frames)], lat_sem.at[g])

    def far_arrive(g):
        drain(lat.at[g, pl.ds(0, part_frames)], lat_sem.at[groups + g])

    def latent(g, r):
        x = lat[g, r * slab_frames : (r + 1) * slab_frames].astype(jnp.float32)
        return x.reshape(slab, width)

    def prepare(g, r, at):
        n = layer_norm(latent(g, r))
        for c in range(n_cfg):
            y = n * (1.0 + modulation(c, 1)) + modulation(c, 0)
            start = at + c * part_rows + (r % 2) * slab
            normed[start : start + slab, :] = y.astype(jnp.bfloat16)

    def project(owners, first, j):
        x = normed[: len(owners) * n_cfg * part_rows]
        for part in range(3):
            at = slice(part * width + j * chunk, part * width + (j + 1) * chunk)
            out = jnp.dot(x, wqkv[:, at], preferred_element_type=jnp.float32)
            if part == 0:
                out = out * (1.0 / math.sqrt(head_dim))
            out = out.astype(jnp.bfloat16)
            for n, g in enumerate(owners):
                for c in range(n_cfg):
                    start = (n * n_cfg + c) * part_rows
                    qkv[g, c, first : first + part_rows, at] = out[start : start + part_rows]

    def attend(g, c, h):
        at = slice(c * rows, (c + 1) * rows)
        kk = qkv[g, c, :, width + h * pair : width + (h + 1) * pair]
        vv = qkv[g, c, :, 2 * width + h * pair : 2 * width + (h + 1) * pair]
        keys = jnp.concatenate([kk * left, kk * right], axis=0)
        vals = jnp.concatenate([vv * left, vv * right], axis=0)
        vals = jnp.concatenate([vals, shares], axis=1)
        scores = lax.dot_general(
            qkv[g, c, :, h * pair : (h + 1) * pair], keys, (((1,), (1,)), ((), ())),
            preferred_element_type=jnp.float32,
        )
        probs = []
        for s in range(2):
            t = scores[:, s * rows : (s + 1) * rows].reshape(all_frames, GROUP, rows)
            t = jnp.where(same, t, -jnp.inf).reshape(rows, rows)
            e = jnp.exp(t - jnp.max(t, axis=1, keepdims=True))
            probs.append(e.astype(jnp.bfloat16))
        both = jnp.dot(
            jnp.concatenate(probs, axis=1), vals, preferred_element_type=jnp.float32
        )
        o = both[:, :pair] / both[:, pair:]
        mixed[at, h * pair : (h + 1) * pair] = o.astype(jnp.bfloat16)

    def leave(j):
        at = slice(j * chunk, (j + 1) * chunk)
        branch[:, at] = jnp.dot(mixed[...], wo[:, at], preferred_element_type=jnp.float32)

    def settle(g, r):
        x = latent(g, r)
        for c in range(n_cfg):
            start = c * rows + r * slab
            residual = x + modulation(c, 2) * branch[start : start + slab, :]
            final = layer_norm(residual) * (1.0 + modulation(c, 4)) + modulation(c, 3)
            finals[start : start + slab, :] = final.astype(jnp.bfloat16)

    def guide():
        both = lax.dot_general(
            finals[...], wh[...], (((1,), (1,)), ((), ())), preferred_element_type=jnp.float32
        )
        guided = both[rows:] + guide_scale * (both[:rows] - both[rows:])
        spare[...] = guided.reshape(all_frames, GROUP, PACK * out_ch).astype(spare.dtype)

    def give(g):
        q = g // PACK

        @pl.when(lax.rem(g, PACK) == 0)
        def _():
            preds[q] = spare[...]

        @pl.when(lax.rem(g, PACK) != 0)
        def _():
            preds[q, :, :, out_ch:] = spare[:, :, out_ch:]

        @pl.when((lax.rem(g, PACK) == PACK - 1) | (g == groups - 1))
        def _():
            each(1, total, lambda k: ret_copy(q, k).start())
            landed[q, mine] = preds[q, pl.ds(place(me, side), frames)]

    def attention(g):
        def one(n, carry):
            for c in range(n_cfg):
                for h in range(width // pair):
                    attend(g, c, h)
            return carry

        lax.fori_loop(0, 1, one, 0)

    def near_wave(b, carry):
        owners = [b * batch + n for n in range(batch)]
        for g in owners:
            near_arrive(g)
        for n, g in enumerate(owners):
            for r in range(2):
                prepare(g, r, n * n_cfg * part_rows)
        for j in range(steps):
            project(owners, 0, j)

        @pl.when(AHEAD + b < groups)
        def _():
            send_far(AHEAD + b, 0, half_seq * (1 - edge))
        return carry
    lax.fori_loop(0, groups // batch, near_wave, 0)
    for g in range(AHEAD + groups // batch, groups):
        send_far(g, 0, half_seq * (1 - edge))

    def far_wave(g, late):
        far_arrive(g)
        for r in range(2, 4):
            prepare(g, r, 0)
        for j in range(steps):
            project([g], part_rows, j)
            if j < len(late):
                late[j]()
        attention(g)

    def leave_all():
        for j in range(steps):
            leave(j)

    far_wave(jnp.int32(0), [])
    leave_all()

    def wave(g, carry):
        far_wave(g, [functools.partial(settle, g - 1, r) for r in range(4)] + [guide])
        give(g - 1)
        leave_all()
        return carry

    lax.fori_loop(1, groups, wave, 0)
    for r in range(4):
        settle(groups - 1, r)
    guide()
    give(jnp.int32(groups - 1))
    drain(slots.at[pl.ds(0, n_seq - 1)], msg_sem.at[0])
    drain(mods.at[pl.ds(0, total - 1)], mod_sem.at[0])
    drain(lat.at[:, pl.ds(0, all_frames - frames)], lat_sem.at[2 * groups])
    for q in range(pairs):
        drain(landed.at[q, pl.ds(0, total - 1)], ret_recv.at[q])
        drain(landed.at[q, pl.ds(0, total - 1)], ret_send.at[q])
    per = 128 // GROUP
    for f in range(frames):
        slabs = []
        for source in range(total):
            for g in range(groups):
                tile = landed[g // PACK, source, f].astype(jnp.float32)
                if g % PACK:
                    tile = pltpu.roll(tile, out_ch, 1)
                slabs.append(tile)
        for n in range(pixels // 128):
            block = jnp.concatenate(slabs[n * per : (n + 1) * per], axis=0)
            out_ref[f, :, n * 128 : (n + 1) * 128] = block.T[:out_ch]


def whole(step, num, den, ids, latent, table, tin, tout, mod_w, wqkv, wo, wh):
    n_cfg, n_seq = lax.axis_size("cfg"), lax.axis_size("seq")
    frames, pixels, width = latent.shape
    head_dim = width // HEADS
    items = pixels // n_cfg // n_seq
    groups, all_frames = items // GROUP, frames * n_seq
    rows = all_frames * GROUP
    total = n_cfg * n_seq
    pairs = -(-groups // PACK)
    mod_cols = mod_w.shape[0]
    out_ch = wh.shape[0]
    hbm = pl.BlockSpec(memory_space=pl.ANY)
    bf16 = jnp.bfloat16
    dma = pltpu.SemaphoreType.DMA
    return pl.pallas_call(
        functools.partial(whole_kernel, n_cfg, n_seq, head_dim),
        out_shape=pltpu.VMEM((frames, out_ch, pixels), jnp.float32),
        in_specs=[pl.BlockSpec(memory_space=pltpu.HBM)] * 3 + [hbm] * 9,
        out_specs=pl.BlockSpec(memory_space=pltpu.VMEM),
        scratch_shapes=[
            pltpu.SMEM((1,), jnp.int32),
            pltpu.SMEM((1,), jnp.int32),
            pltpu.SMEM((1,), jnp.int32),
            pltpu.VMEM(ids.shape, jnp.int32),
            pltpu.VMEM(table.shape, bf16),
            pltpu.VMEM(tin.shape, bf16),
            pltpu.VMEM(tout.shape, bf16),
            pltpu.VMEM(mod_w.shape, bf16),
            pltpu.VMEM(wqkv.shape, bf16),
            pltpu.VMEM(wo.shape, bf16),
            pltpu.VMEM((PACK * out_ch, width), bf16),
            pltpu.VMEM((groups, all_frames, GROUP, width), bf16),
            pltpu.VMEM((n_seq, 2, width // 2), bf16),
            pltpu.VMEM((total, 1, mod_cols), jnp.float32),
            pltpu.VMEM((n_cfg, n_seq * mod_cols), jnp.float32),
            pltpu.VMEM((min(2, groups) * n_cfg * rows // 2, width), bf16),
            pltpu.VMEM((groups, n_cfg, rows, 3 * width), bf16),
            pltpu.VMEM((n_cfg * rows, width), bf16),
            pltpu.VMEM((n_cfg * rows, width), jnp.float32),
            pltpu.VMEM((n_cfg * rows, width), bf16),
            pltpu.VMEM((all_frames, GROUP, PACK * out_ch), bf16),
            pltpu.VMEM((pairs, all_frames, GROUP, PACK * out_ch), bf16),
            pltpu.VMEM((pairs, total, frames, GROUP, PACK * out_ch), bf16),
            dma((11 + -(-table.shape[0] // SLICE),)), dma((2,)), dma((2,)), dma((groups,)),
            dma((2 * groups + 1,)), dma((pairs,)), dma((pairs,)),
        ],
        compiler_params=pltpu.CompilerParams(
            collective_id=0, has_side_effects=True, vmem_limit_bytes=VMEM_BYTES
        ),
        name="whole",
    )(step, num, den, ids, latent, table, tin, tout, mod_w, wqkv, wo, wh)


def on_device(
    latent, text_ids, timestep, guide_num, guide_den, text_table,
    time_in, time_out, mod_weight, qkv_weight, out_weight, head_weight,
):
    out = whole(
        timestep, guide_num, guide_den, text_ids, latent,
        text_table, time_in, time_out.T, mod_weight.T, qkv_weight, out_weight, head_weight.T,
    )
    return jnp.swapaxes(out, 1, 2)


def solution(mesh):
    in_specs = (
        P("seq", None, None), P("cfg", None), P(), P(), P(), P("seq", None),
        P(), P(None, "seq"), P(None, "seq"), P(), P(), P(),
    )
    return jax.shard_map(
        on_device, mesh=mesh, in_specs=in_specs, out_specs=P("seq", None, None), check_vma=False
    )
```

time: 74.7 us -> 61.4 us (0.82)
  Pallas kernels: 70.9 us -> 58.5 us
  local copies, waits for them, and re-layouts: 1.67 us -> 0.71 us
    pallas_call x1, Pallas kernels: 70.9 us -> 58.5 us  [whole(): pl.pallas_call(functools.partial(whole_kernel, n_cfg, n_seq, head_dim), o...]
    unnamed x1, local copies, waits for them, and re-layouts: 1.67 us -> 0.71 us
where the time goes in v2:
time: 61.4 us; the launch traced here: 61.2 us
  Pallas kernels  58.5 us (95%)
  between operations  1.95 us (3%)
  local copies, waits for them, and re-layouts  0.71 us (1%)
    pallas_call x1, Pallas kernels, whole(): pl.pallas_call(functools.partial(whole_kernel, n_cfg, n_seq, head_dim), o...  58.5 us

profile of v2, /device:TPU:0, one launch (start us, length us, event | category | flops | bytes accessed | tf_op | source)
XLA Modules:
  0.0 61.2 jit_solution(7420867142754166570)
XLA Ops:
  1.9 58.5 %whole.1 = f32[1,64,1024]{2,1,0:T(8,128)S(1)} custom-call(s32[1]{0:T(128)S(6)} %copy.15.step_hbm, s32[1]{0:T(128)S(6)} %copy.16.num_hbm, s32[1]{0:T(128)S(6)} %copy.17.den_hbm, s32[1,512]{1,0:T(1,128)} %ids_hbm.1, bf16[1,1024,1536]{2,1,0:T(8,128)(2,1)} %latent_ref.1, bf16[2008,1536]{1,0:T(8,128)(2,1)} %table_hbm.1, bf16[256,1536]{1,0:T(8,128)(2,1)} %tin_hbm.1, ...), custom_call_target="tpu_custom_call" | custom-call | tf_op jit(solution)/shard_map/whole/pallas_call | solution.py:421
  60.5 0.7 %copy.14 = f32[1,1024,64]{1,2,0:T(8,128)} copy(f32[1,1024,64]{1,2,0:T(8,128)S(1)} %bitcast.4) | data formatting | bytes 524288

commit v3 on v2

--- a/solution.py
+++ b/solution.py
@@ -13,10 +13,6 @@
 NORM_FLOOR = 0.1
 GROUP = 8
 PACK = 2
-EDGE_EARLY = 5
-MIDDLE_EARLY = 8
-AHEAD = 2
-NEAR_EARLY = 2
 SLICE = 512
 VMEM_BYTES = 60 * 1024 * 1024
 MESH = pl.DeviceIdType.MESH
@@ -38,6 +34,14 @@
         return carry
 
     lax.fori_loop(low, high, run, 0)
+
+
+def many(low, high, act):
+    def run(k, carry):
+        act(k)
+        return carry
+
+    lax.fori_loop(low, high, run, 0, unroll=True)
 
 
 def whole_kernel(
@@ -53,7 +57,6 @@
     half_seq = n_seq // 2
     side, spot = me // half_seq, lax.rem(me, half_seq)
     edge = jnp.where((2 * me // half_seq == 0) | (2 * me // half_seq == 3), 1, 0)
-    early = min(MIDDLE_EARLY, half_seq) + edge * (min(EDGE_EARLY, half_seq) - min(MIDDLE_EARLY, half_seq))
     frames, pixels, width = latent_ref.shape
     items = pixels // n_cfg // n_seq
     groups, all_frames = lat.shape[0], lat.shape[1]
@@ -113,7 +116,7 @@
         )
 
     def far_copy(g, k):
-        peer = (1 - side) * half_seq + lax.rem(spot + k, half_seq)
+        peer = (1 - side) * half_seq + lax.rem(spot + k + half_seq // 2, half_seq)
         return pltpu.make_async_remote_copy(
             src_ref=piece(peer, g), dst_ref=lat.at[g, pl.ds(place(me, 1 - side), frames)],
             send_sem=lat_sem.at[2 * groups], recv_sem=lat_sem.at[groups + g],
@@ -125,9 +128,19 @@
             piece(me, g), lat.at[g, pl.ds(place(me, side), frames)], own_sem.at[g]
         )
 
-    def send_near(g):
-        own_copy(g).start()
-        each(1, half_seq, lambda k: near_copy(g, k).start())
+    def volley(nears, fars, on):
+        nears = [g for g in nears if g < groups]
+        fars = [g for g in fars if g < groups]
+
+        def shot(k):
+            for g in nears:
+                near_copy(g, k).start()
+            for g in fars:
+                far_copy(g, k).start()
+
+        for g in fars:
+            send_far(g, 0, on)
+        each(1, 1 + (half_seq - 1) * on, shot)
 
     def send_far(g, low, high):
         each(low, high, lambda k: far_copy(g, k).start())
@@ -191,26 +204,25 @@
     for n in range(4, 11):
         loads[n].start()
     pooled = jnp.sum(sums, axis=0, keepdims=True) * (1.0 / math.sqrt(tokens)) + placed
-    wide = width // 2
-    slots[me] = jnp.concatenate([pooled[:, :wide], pooled[:, wide:]], axis=0).astype(slots.dtype)
+    slots[me] = pooled
     pl.semaphore_wait(barrier, total - 1)
-    each(1, n_seq, lambda k: msg_copy(k).start())
-    for g in range(min(NEAR_EARLY, groups)):
-        send_near(g)
-    send_far(0, 0, early)
+    many(1, n_seq, lambda k: msg_copy(k).start())
+    for g in range(groups):
+        own_copy(g).start()
+    volley([0, 1], [], edge)
+    volley([0], [0], 1 - edge)
+    volley([1], [], 1 - edge)
     loads[4].wait()
     drain(slots.at[pl.ds(0, n_seq - 1)], msg_sem.at[1])
-    cond = silu(jnp.sum(slots[...].astype(jnp.float32), axis=0)).astype(jnp.bfloat16)
-    cond = jnp.concatenate([cond[:1], cond[1:]], axis=1)
+    cond = silu(jnp.sum(slots[...], axis=0)).astype(jnp.bfloat16)
     mods[mine] = lax.dot_general(
         cond, mod_w[...], (((1,), (1,)), ((), ())), preferred_element_type=jnp.float32
     )
-    each(1, total, lambda k: mod_copy(k).start())
-    for g in range(min(NEAR_EARLY, groups), groups):
-        send_near(g)
-    send_far(0, early, half_seq)
-    for g in range(1, groups):
-        send_far(g, 0, half_seq if g < AHEAD else half_seq * edge)
+    many(1, total, lambda k: mod_copy(k).start())
+    volley([2, 3], [], edge)
+    send_far(0, 0, half_seq * edge)
+    volley([], [1], edge)
+    volley([2, 3], [1], 1 - edge)
     for n in range(5, 11):
         loads[n].wait()
     drain(mods.at[pl.ds(0, total - 1)], mod_sem.at[1])
@@ -272,7 +284,6 @@
                     qkv[g, c, first : first + part_rows, at] = out[start : start + part_rows]
 
     def attend(g, c, h):
-        at = slice(c * rows, (c + 1) * rows)
         kk = qkv[g, c, :, width + h * pair : width + (h + 1) * pair]
         vv = qkv[g, c, :, 2 * width + h * pair : 2 * width + (h + 1) * pair]
         keys = jnp.concatenate([kk * left, kk * right], axis=0)
@@ -292,26 +303,51 @@
             jnp.concatenate(probs, axis=1), vals, preferred_element_type=jnp.float32
         )
         o = both[:, :pair] / both[:, pair:]
-        mixed[at, h * pair : (h + 1) * pair] = o.astype(jnp.bfloat16)
-
-    def leave(j):
+        o = o.astype(jnp.bfloat16)
+        for part in range(2):
+            start = (part * n_cfg + c) * part_rows
+            mixed[start : start + part_rows, h * pair : (h + 1) * pair] = o[
+                part * part_rows : (part + 1) * part_rows
+            ]
+
+    def leave(part, j):
         at = slice(j * chunk, (j + 1) * chunk)
-        branch[:, at] = jnp.dot(mixed[...], wo[:, at], preferred_element_type=jnp.float32)
+        block = slice(part * rows, (part + 1) * rows)
+        branch[block, at] = jnp.dot(mixed[block, :], wo[:, at], preferred_element_type=jnp.float32)
 
     def settle(g, r):
         x = latent(g, r)
         for c in range(n_cfg):
-            start = c * rows + r * slab
+            start = (r // 2 * n_cfg + c) * part_rows + r % 2 * slab
             residual = x + modulation(c, 2) * branch[start : start + slab, :]
             final = layer_norm(residual) * (1.0 + modulation(c, 4)) + modulation(c, 3)
             finals[start : start + slab, :] = final.astype(jnp.bfloat16)
 
-    def guide():
+    def guide(part):
+        block = slice(part * rows, (part + 1) * rows)
         both = lax.dot_general(
-            finals[...], wh[...], (((1,), (1,)), ((), ())), preferred_element_type=jnp.float32
-        )
-        guided = both[rows:] + guide_scale * (both[:rows] - both[rows:])
-        spare[...] = guided.reshape(all_frames, GROUP, PACK * out_ch).astype(spare.dtype)
+            finals[block, :], wh[...], (((1,), (1,)), ((), ())), preferred_element_type=jnp.float32
+        )
+        guided = both[part_rows:] + guide_scale * (both[:part_rows] - both[part_rows:])
+        spare[part * part_frames : (part + 1) * part_frames] = guided.reshape(
+            part_frames, GROUP, PACK * out_ch
+        ).astype(spare.dtype)
+
+    def finish(g):
+        for j in range(steps):
+            leave(0, j)
+        for j in range(steps):
+            leave(1, j)
+            if j in (1, 3):
+                settle(g, j // 2)
+        guide(0)
+        settle(g, 2)
+        settle(g, 3)
+        guide(1)
+
+    def send_pair(q):
+        many(1, total, lambda k: ret_copy(q, k).start())
+        landed[q, mine] = preds[q, pl.ds(place(me, side), frames)]
 
     def give(g):
         q = g // PACK
@@ -324,10 +360,13 @@
         def _():
             preds[q, :, :, out_ch:] = spare[:, :, out_ch:]
 
-        @pl.when((lax.rem(g, PACK) == PACK - 1) | (g == groups - 1))
+        @pl.when((lax.rem(g, PACK) == 0) & (g > 0))
         def _():
-            each(1, total, lambda k: ret_copy(q, k).start())
-            landed[q, mine] = preds[q, pl.ds(place(me, side), frames)]
+            send_pair(q - 1)
+
+        @pl.when(g == groups - 1)
+        def _():
+            send_pair(q)
 
     def attention(g):
         def one(n, carry):
@@ -348,42 +387,26 @@
         for j in range(steps):
             project(owners, 0, j)
 
-        @pl.when(AHEAD + b < groups)
+        @pl.when(2 + b < groups)
         def _():
-            send_far(AHEAD + b, 0, half_seq * (1 - edge))
+            send_far(2 + b, 0, half_seq)
         return carry
     lax.fori_loop(0, groups // batch, near_wave, 0)
-    for g in range(AHEAD + groups // batch, groups):
-        send_far(g, 0, half_seq * (1 - edge))
-
-    def far_wave(g, late):
+    for g in range(2 + groups // batch, groups):
+        send_far(g, 0, half_seq)
+
+    def far_wave(g, carry):
         far_arrive(g)
         for r in range(2, 4):
             prepare(g, r, 0)
         for j in range(steps):
             project([g], part_rows, j)
-            if j < len(late):
-                late[j]()
         attention(g)
-
-    def leave_all():
-        for j in range(steps):
-            leave(j)
-
-    far_wave(jnp.int32(0), [])
-    leave_all()
-
-    def wave(g, carry):
-        far_wave(g, [functools.partial(settle, g - 1, r) for r in range(4)] + [guide])
-        give(g - 1)
-        leave_all()
+        finish(g)
+        give(g)
         return carry
 
-    lax.fori_loop(1, groups, wave, 0)
-    for r in range(4):
-        settle(groups - 1, r)
-    guide()
-    give(jnp.int32(groups - 1))
+    lax.fori_loop(0, groups, far_wave, 0)
     drain(slots.at[pl.ds(0, n_seq - 1)], msg_sem.at[0])
     drain(mods.at[pl.ds(0, total - 1)], mod_sem.at[0])
     drain(lat.at[:, pl.ds(0, all_frames - frames)], lat_sem.at[2 * groups])
@@ -436,7 +459,7 @@
             pltpu.VMEM(wo.shape, bf16),
             pltpu.VMEM((PACK * out_ch, width), bf16),
             pltpu.VMEM((groups, all_frames, GROUP, width), bf16),
-            pltpu.VMEM((n_seq, 2, width // 2), bf16),
+            pltpu.VMEM((n_seq, 1, width), jnp.float32),
             pltpu.VMEM((total, 1, mod_cols), jnp.float32),
             pltpu.VMEM((n_cfg, n_seq * mod_cols), jnp.float32),
             pltpu.VMEM((min(2, groups) * n_cfg * rows // 2, width), bf16),

time: 61.4 us -> 60.9 us (level)
  no operation moved by 1% of the time
where the time goes in v3:
time: 60.9 us; the launch traced here: 60.7 us
  Pallas kernels  58 us (95%)
  between operations  1.95 us (3%)
  local copies, waits for them, and re-layouts  0.71 us (1%)
    pallas_call x1, Pallas kernels, whole(): pl.pallas_call(functools.partial(whole_kernel, n_cfg, n_seq, head_dim), o...  58 us

profile of v3, /device:TPU:0, one launch (start us, length us, event | category | flops | bytes accessed | tf_op | source)
XLA Modules:
  0.0 60.7 jit_solution(15434838603082142217)
XLA Ops:
  1.9 58.0 %whole.1 = f32[1,64,1024]{2,1,0:T(8,128)S(1)} custom-call(s32[1]{0:T(128)S(6)} %copy.15.step_hbm, s32[1]{0:T(128)S(6)} %copy.16.num_hbm, s32[1]{0:T(128)S(6)} %copy.17.den_hbm, s32[1,512]{1,0:T(1,128)} %ids_hbm.1, bf16[1,1024,1536]{2,1,0:T(8,128)(2,1)} %latent_ref.1, bf16[2008,1536]{1,0:T(8,128)(2,1)} %table_hbm.1, bf16[256,1536]{1,0:T(8,128)(2,1)} %tin_hbm.1, ...), custom_call_target="tpu_custom_call" | custom-call | tf_op jit(solution)/shard_map/whole/pallas_call | solution.py:444
  60.0 0.7 %copy.14 = f32[1,1024,64]{1,2,0:T(8,128)} copy(f32[1,1024,64]{1,2,0:T(8,128)S(1)} %bitcast.4) | data formatting | bytes 524288
